TPU v7x, 32 devices: a whole 2x2x4 slice. The times are simulated.
32 devices in a mesh: grp: 2 (over y), row: 16 (over z, x, core).
Axes of the slice: x: 2, y: 2, z: 4, core: 2. Of those that a mesh axis runs over, the one named last changes fastest.
Arguments:
- diag_blocks: float32 [8192, 512], P('row'), may hold values from -0.6 to 2.6
- lower_coupling: float32 [8192, 64], P('row'), may hold values from -0.3125 to 0.3125
- upper_coupling: float32 [8192, 64], P('row'), may hold values from -0.3125 to 0.3125
- right_sides: float32 [8192, 1024], P('row', 'grp'), parts along dimension 1, may hold values from -108 to 108
Outputs:
- solution: float32 [8192, 1024], P('row', 'grp'), parts along dimension 1
- res_norms: float32 [8, 1024], P(None, 'grp'), parts along dimension 1
There are 2 independent parts, one for each index of `grp`. A program takes and returns all parts, laid end to end along the dimension named above; an argument that names none is the same for every part. Nothing has to cross between parts.
All inputs are finite; a program needn't handle non-finite values.
Results may differ from a plain program's by a relative error of at most 0.0001.
Values sent between devices are 32-bit elements; how exact they have to be, the bound alone decides.
A program may use at most 64 MiB of HBM per device.

v0:
```python
import jax
import jax.numpy as jnp
from jax import lax
from jax.sharding import PartitionSpec as P

SWEEPS = 8


def extended(shard, sides, width):
    for axis, dim in sides:
        size, length = (lax.axis_size(axis), shard.shape[dim])
        up = [(i, (i + 1) % size) for i in range(size - 1)]
        down = [(j, i) for i, j in up]
        last = lax.slice_in_dim(shard, length - width, length, axis=dim)
        first = lax.slice_in_dim(shard, 0, width, axis=dim)
        before = lax.ppermute(last, axis, up)
        after = lax.ppermute(first, axis, down)
        shard = jnp.concatenate([before, shard, after], axis=dim)
    return shard


def matmul(left, right):
    return jnp.dot(left, right, precision=lax.Precision.HIGHEST, preferred_element_type=jnp.float32)


def local(diag_blocks, lower_coupling, upper_coupling, right_sides):
    pivots = jnp.diagonal(diag_blocks)[:, None]
    width = lower_coupling.shape[1]
    solution = jnp.zeros_like(right_sides)
    partials = []
    for sweep_index in range(SWEEPS):
        padded = extended(solution, (("row", 0),), width)
        before = padded[:width]
        after = padded[padded.shape[0] - width :]
        images = (
            matmul(diag_blocks, solution)
            + matmul(lower_coupling, before)
            + matmul(upper_coupling, after)
        )
        residual = right_sides - images
        local_sums = jnp.sum(residual * residual, axis=0)
        solution = solution + residual / pivots
        partials.append(local_sums)
    res_norms = jnp.sqrt(lax.psum(jnp.stack(partials), "row"))
    return (solution, res_norms)


def solution(mesh):
    return jax.shard_map(
        local,
        mesh=mesh,
        in_specs=(P("row", None), P("row", None), P("row", None), P("row", "grp")),
        out_specs=(P("row", "grp"), P(None, "grp")),
        check_vma=False,
    )
```

profile of v0, /device:TPU:0, one launch (start us, length us, event | category | flops | bytes accessed | tf_op | source)
XLA Modules:
  0.0 163.6 jit_solution(15000186278195526279)
XLA Ops:
  0.7 1.4 collective-permute-start.1
  2.1 3.0 %collective-permute-start = (f32[64,512]{1,0:T(8,128)S(1)}, f32[64,512]{1,0:T(8,128)S(1)}, u32[]{:S(2)}, u32[]{:S(2)}) collective-permute-start(f32[64,512]{1,0:T(8,128)S(1)} %broadcast.16), channel_id=1, source_target_pairs={{0,1},{1,2},{2,3},{3,4},{4,5},{5,6},{6,7},{7,8},{8,9},{9,10},{10,1... | collective-permute-start | bytes 393224 | tf_op jit(solution)/shard_map/ppermute | solution.py:16
  5.2 8.5 %gather_fusion = f32[512]{0:T(512)S(1)} fusion(f32[512,512]{1,0:T(8,128)} %param.4, s32[512]{0:T(512)S(1)} %bitcast.87), kind=kCustom, calls=%fused_computation | custom fusion | bytes 8192 | tf_op jit(solution)/shard_map/jit(diagonal)/cond/branch_0_fun/gather | solution.py:27
  14.9 1.2 multiply_reduce_fusion.7
  16.1 4.5 %collective-permute-start.2 = (f32[64,512]{1,0:T(8,128)S(1)}, f32[64,512]{1,0:T(8,128)S(1)}, u32[]{:S(2)}, u32[]{:S(2)}) collective-permute-start(f32[64,512]{1,0:T(8,128)S(1)} %get-tuple-element.31), channel_id=1, source_target_pairs={{0,1},{1,2},{2,3},{3,4},{4,5},{5,6},{6,7},{7,8},{8,9},{9,10},{10,1... | collective-permute-start | bytes 393224 | tf_op jit(solution)/shard_map/ppermute | solution.py:16
  20.6 1.9 %fusion.25 = f32[512,512]{0,1:T(8,128)S(1)} fusion(f32[512,512]{1,0:T(8,128)S(1)} %get-tuple-element.17, f32[512,512]{1,0:T(8,128)S(1)} %copy-done.1), kind=kOutput, calls=%fused_computation.59 | convolution fusion | flops 1610612736 | bytes 3145728 | tf_op jit(solution)/shard_map/dot_general | solution.py:23
  22.5 1.3 collective-permute-start.3
  25.8 1.2 multiply_reduce_fusion.6
  27.0 5.7 %collective-permute-start.4 = (f32[64,512]{1,0:T(8,128)S(1)}, f32[64,512]{1,0:T(8,128)S(1)}, u32[]{:S(2)}, u32[]{:S(2)}) collective-permute-start(f32[64,512]{1,0:T(8,128)S(1)} %get-tuple-element.29), channel_id=1, source_target_pairs={{0,1},{1,2},{2,3},{3,4},{4,5},{5,6},{6,7},{7,8},{8,9},{9,10},{10,1... | collective-permute-start | bytes 393224 | tf_op jit(solution)/shard_map/ppermute | solution.py:16
  32.7 1.9 %fusion.26 = f32[512,512]{0,1:T(8,128)S(1)} fusion(f32[512,512]{1,0:T(8,128)S(1)} %get-tuple-element.15, f32[512,512]{1,0:T(8,128)S(1)} %copy-done.1), kind=kOutput, calls=%fused_computation.60 | convolution fusion | flops 1610612736 | bytes 3145728 | tf_op jit(solution)/shard_map/dot_general | solution.py:23
  34.6 1.3 collective-permute-start.5
  37.8 1.2 multiply_reduce_fusion.5
  39.0 6.0 %collective-permute-start.6 = (f32[64,512]{1,0:T(8,128)S(1)}, f32[64,512]{1,0:T(8,128)S(1)}, u32[]{:S(2)}, u32[]{:S(2)}) collective-permute-start(f32[64,512]{1,0:T(8,128)S(1)} %get-tuple-element.27), channel_id=1, source_target_pairs={{0,1},{1,2},{2,3},{3,4},{4,5},{5,6},{6,7},{7,8},{8,9},{9,10},{10,1... | collective-permute-start | bytes 393224 | tf_op jit(solution)/shard_map/ppermute | solution.py:16
  45.1 1.9 %fusion.27 = f32[512,512]{0,1:T(8,128)S(1)} fusion(f32[512,512]{1,0:T(8,128)S(1)} %get-tuple-element.13, f32[512,512]{1,0:T(8,128)S(1)} %copy-done.1), kind=kOutput, calls=%fused_computation.61 | convolution fusion | flops 1610612736 | bytes 3145728 | tf_op jit(solution)/shard_map/dot_general | solution.py:23
  47.0 1.3 collective-permute-start.7
  51.4 5.9 %collective-permute-start.8 = (f32[64,512]{1,0:T(8,128)S(1)}, f32[64,512]{1,0:T(8,128)S(1)}, u32[]{:S(2)}, u32[]{:S(2)}) collective-permute-start(f32[64,512]{1,0:T(8,128)S(1)} %get-tuple-element.25), channel_id=1, source_target_pairs={{0,1},{1,2},{2,3},{3,4},{4,5},{5,6},{6,7},{7,8},{8,9},{9,10},{10,1... | collective-permute-start | bytes 393224 | tf_op jit(solution)/shard_map/ppermute | solution.py:16
  57.3 1.9 %fusion.28 = f32[512,512]{0,1:T(8,128)S(1)} fusion(f32[512,512]{1,0:T(8,128)S(1)} %get-tuple-element.11, f32[512,512]{1,0:T(8,128)S(1)} %copy-done.1), kind=kOutput, calls=%fused_computation.62 | convolution fusion | flops 1610612736 | bytes 3145728 | tf_op jit(solution)/shard_map/dot_general | solution.py:23
  59.2 1.3 collective-permute-start.9
  62.4 1.2 multiply_reduce_fusion.3
  63.6 5.9 %collective-permute-start.10 = (f32[64,512]{1,0:T(8,128)S(1)}, f32[64,512]{1,0:T(8,128)S(1)}, u32[]{:S(2)}, u32[]{:S(2)}) collective-permute-start(f32[64,512]{1,0:T(8,128)S(1)} %get-tuple-element.23), channel_id=1, source_target_pairs={{0,1},{1,2},{2,3},{3,4},{4,5},{5,6},{6,7},{7,8},{8,9},{9,10},{10,1... | collective-permute-start | bytes 393224 | tf_op jit(solution)/shard_map/ppermute | solution.py:16
  69.5 1.9 %fusion.29 = f32[512,512]{0,1:T(8,128)S(1)} fusion(f32[512,512]{1,0:T(8,128)S(1)} %get-tuple-element.9, f32[512,512]{1,0:T(8,128)S(1)} %copy-done.1), kind=kOutput, calls=%fused_computation.63 | convolution fusion | flops 1610612736 | bytes 3145728 | tf_op jit(solution)/shard_map/dot_general | solution.py:23
  71.4 1.3 collective-permute-start.11
  74.6 1.2 multiply_reduce_fusion.2
  75.9 6.1 %collective-permute-start.12 = (f32[64,512]{1,0:T(8,128)S(1)}, f32[64,512]{1,0:T(8,128)S(1)}, u32[]{:S(2)}, u32[]{:S(2)}) collective-permute-start(f32[64,512]{1,0:T(8,128)S(1)} %get-tuple-element.21), channel_id=1, source_target_pairs={{0,1},{1,2},{2,3},{3,4},{4,5},{5,6},{6,7},{7,8},{8,9},{9,10},{10,1... | collective-permute-start | bytes 393224 | tf_op jit(solution)/shard_map/ppermute | solution.py:16
  82.0 1.9 %fusion.30 = f32[512,512]{0,1:T(8,128)S(1)} fusion(f32[512,512]{1,0:T(8,128)S(1)} %get-tuple-element.7, f32[512,512]{1,0:T(8,128)S(1)} %copy-done.1), kind=kOutput, calls=%fused_computation.64 | convolution fusion | flops 1610612736 | bytes 3145728 | tf_op jit(solution)/shard_map/dot_general | solution.py:23
  83.8 1.3 collective-permute-start.13
  87.1 1.2 multiply_reduce_fusion.1
  88.3 5.9 %collective-permute-start.14 = (f32[64,512]{1,0:T(8,128)S(1)}, f32[64,512]{1,0:T(8,128)S(1)}, u32[]{:S(2)}, u32[]{:S(2)}) collective-permute-start(f32[64,512]{1,0:T(8,128)S(1)} %get-tuple-element.19), channel_id=1, source_target_pairs={{0,1},{1,2},{2,3},{3,4},{4,5},{5,6},{6,7},{7,8},{8,9},{9,10},{10,1... | collective-permute-start | bytes 393224 | tf_op jit(solution)/shard_map/ppermute | solution.py:16
  94.2 1.9 %fusion.31 = f32[512,512]{0,1:T(8,128)S(1)} fusion(f32[512,512]{1,0:T(8,128)S(1)} %get-tuple-element.5, f32[512,512]{1,0:T(8,128)S(1)} %copy-done.1), kind=kOutput, calls=%fused_computation.65 | convolution fusion | flops 1610612736 | bytes 3145728 | tf_op jit(solution)/shard_map/dot_general | solution.py:23
  96.1 1.3 collective-permute-start.15
  99.3 2.2 %multiply_reduce_fusion = (f32[512]{0:T(512)S(1)}, f32[512,512]{1,0:T(8,128)}) fusion(f32[512,512]{1,0:T(8,128)S(1)} %get-tuple-element.5, f32[512]{0:T(512)S(1)} %gather_fusion, f32[512,512]{1,0:T(8,128)S(1)} %copy-done.3, f32[512,512]{0,1:T(8,128)S(1)} %convolution_add_fusion.1, f32[64,512]{1,0:T(8,128)S(1)} %collective-permute-done.15, ...), kind=kOutput, calls=%fused_computation.33 | convolution fusion | flops 202898944 | bytes 4460544 | tf_op jit(solution)/shard_map/dot_general | solution.py:23
  101.5 61.5 %psum.7 = f32[8,512]{1,0:T(8,128)S(1)} all-reduce(f32[8,512]{1,0:T(8,128)S(1)} %stack.35), channel_id=1, replica_groups=mesh['grp'=2,'row'=16] {'row'}, use_global_device_ids=true, to_apply=%region_9.10 | all-reduce | flops 4096 | bytes 32768 | tf_op jit(solution)/shard_map/psum | solution.py:44
  (45 shorter events, 16.7 us)
Async XLA Ops:
  0.6 13.2 %copy-start = (f32[512,64]{0,1:T(8,128)S(1)}, f32[512,64]{0,1:T(8,128)}, u32[]{:S(2)}) copy-start(f32[512,64]{0,1:T(8,128)} %param.6) | copy-start | bytes 393220
  0.7 13.2 %collective-permute-start.1 = (f32[64,512]{1,0:T(8,128)S(1)}, f32[64,512]{1,0:T(8,128)S(1)}, u32[]{:S(2)}, u32[]{:S(2)}) collective-permute-start(f32[64,512]{1,0:T(8,128)S(1)} %broadcast.16), channel_id=1, source_target_pairs={{1,0},{2,1},{3,2},{4,3},{5,4},{6,5},{7,6},{8,7},{9,8},{10,9},{11,1... | collective-permute-start | bytes 393224 | tf_op jit(solution)/shard_map/ppermute | solution.py:17
  2.1 12.8 %collective-permute-start = (f32[64,512]{1,0:T(8,128)S(1)}, f32[64,512]{1,0:T(8,128)S(1)}, u32[]{:S(2)}, u32[]{:S(2)}) collective-permute-start(f32[64,512]{1,0:T(8,128)S(1)} %broadcast.16), channel_id=1, source_target_pairs={{0,1},{1,2},{2,3},{3,4},{4,5},{5,6},{6,7},{7,8},{8,9},{9,10},{10,1... | collective-permute-start | bytes 393224 | tf_op jit(solution)/shard_map/ppermute | solution.py:16
  5.2 8.5 %copy-start.1 = (f32[512,512]{1,0:T(8,128)S(1)}, f32[512,512]{1,0:T(8,128)}, u32[]{:S(2)}) copy-start(f32[512,512]{1,0:T(8,128)} %param.4) | copy-start | bytes 3145732
  13.6 1.2 copy-start.3
  13.8 1.1 copy-start.2
  16.1 7.7 %collective-permute-start.2 = (f32[64,512]{1,0:T(8,128)S(1)}, f32[64,512]{1,0:T(8,128)S(1)}, u32[]{:S(2)}, u32[]{:S(2)}) collective-permute-start(f32[64,512]{1,0:T(8,128)S(1)} %get-tuple-element.31), channel_id=1, source_target_pairs={{0,1},{1,2},{2,3},{3,4},{4,5},{5,6},{6,7},{7,8},{8,9},{9,10},{10,1... | collective-permute-start | bytes 393224 | tf_op jit(solution)/shard_map/ppermute | solution.py:16
  22.5 3.2 %collective-permute-start.3 = (f32[64,512]{1,0:T(8,128)S(1)}, f32[64,512]{1,0:T(8,128)S(1)}, u32[]{:S(2)}, u32[]{:S(2)}) collective-permute-start(f32[64,512]{1,0:T(8,128)S(1)} %get-tuple-element.30), channel_id=1, source_target_pairs={{1,0},{2,1},{3,2},{4,3},{5,4},{6,5},{7,6},{8,7},{9,8},{10,9},{11,1... | collective-permute-start | bytes 393224 | tf_op jit(solution)/shard_map/ppermute | solution.py:17
  27.0 8.9 %collective-permute-start.4 = (f32[64,512]{1,0:T(8,128)S(1)}, f32[64,512]{1,0:T(8,128)S(1)}, u32[]{:S(2)}, u32[]{:S(2)}) collective-permute-start(f32[64,512]{1,0:T(8,128)S(1)} %get-tuple-element.29), channel_id=1, source_target_pairs={{0,1},{1,2},{2,3},{3,4},{4,5},{5,6},{6,7},{7,8},{8,9},{9,10},{10,1... | collective-permute-start | bytes 393224 | tf_op jit(solution)/shard_map/ppermute | solution.py:16
  34.6 3.2 %collective-permute-start.5 = (f32[64,512]{1,0:T(8,128)S(1)}, f32[64,512]{1,0:T(8,128)S(1)}, u32[]{:S(2)}, u32[]{:S(2)}) collective-permute-start(f32[64,512]{1,0:T(8,128)S(1)} %get-tuple-element.28), channel_id=1, source_target_pairs={{1,0},{2,1},{3,2},{4,3},{5,4},{6,5},{7,6},{8,7},{9,8},{10,9},{11,1... | collective-permute-start | bytes 393224 | tf_op jit(solution)/shard_map/ppermute | solution.py:17
  39.0 9.2 %collective-permute-start.6 = (f32[64,512]{1,0:T(8,128)S(1)}, f32[64,512]{1,0:T(8,128)S(1)}, u32[]{:S(2)}, u32[]{:S(2)}) collective-permute-start(f32[64,512]{1,0:T(8,128)S(1)} %get-tuple-element.27), channel_id=1, source_target_pairs={{0,1},{1,2},{2,3},{3,4},{4,5},{5,6},{6,7},{7,8},{8,9},{9,10},{10,1... | collective-permute-start | bytes 393224 | tf_op jit(solution)/shard_map/ppermute | solution.py:16
  47.0 3.2 %collective-permute-start.7 = (f32[64,512]{1,0:T(8,128)S(1)}, f32[64,512]{1,0:T(8,128)S(1)}, u32[]{:S(2)}, u32[]{:S(2)}) collective-permute-start(f32[64,512]{1,0:T(8,128)S(1)} %get-tuple-element.26), channel_id=1, source_target_pairs={{1,0},{2,1},{3,2},{4,3},{5,4},{6,5},{7,6},{8,7},{9,8},{10,9},{11,1... | collective-permute-start | bytes 393224 | tf_op jit(solution)/shard_map/ppermute | solution.py:17
  51.4 9.1 %collective-permute-start.8 = (f32[64,512]{1,0:T(8,128)S(1)}, f32[64,512]{1,0:T(8,128)S(1)}, u32[]{:S(2)}, u32[]{:S(2)}) collective-permute-start(f32[64,512]{1,0:T(8,128)S(1)} %get-tuple-element.25), channel_id=1, source_target_pairs={{0,1},{1,2},{2,3},{3,4},{4,5},{5,6},{6,7},{7,8},{8,9},{9,10},{10,1... | collective-permute-start | bytes 393224 | tf_op jit(solution)/shard_map/ppermute | solution.py:16
  59.2 3.2 %collective-permute-start.9 = (f32[64,512]{1,0:T(8,128)S(1)}, f32[64,512]{1,0:T(8,128)S(1)}, u32[]{:S(2)}, u32[]{:S(2)}) collective-permute-start(f32[64,512]{1,0:T(8,128)S(1)} %get-tuple-element.24), channel_id=1, source_target_pairs={{1,0},{2,1},{3,2},{4,3},{5,4},{6,5},{7,6},{8,7},{9,8},{10,9},{11,1... | collective-permute-start | bytes 393224 | tf_op jit(solution)/shard_map/ppermute | solution.py:17
  63.6 9.1 %collective-permute-start.10 = (f32[64,512]{1,0:T(8,128)S(1)}, f32[64,512]{1,0:T(8,128)S(1)}, u32[]{:S(2)}, u32[]{:S(2)}) collective-permute-start(f32[64,512]{1,0:T(8,128)S(1)} %get-tuple-element.23), channel_id=1, source_target_pairs={{0,1},{1,2},{2,3},{3,4},{4,5},{5,6},{6,7},{7,8},{8,9},{9,10},{10,1... | collective-permute-start | bytes 393224 | tf_op jit(solution)/shard_map/ppermute | solution.py:16
  71.4 3.2 %collective-permute-start.11 = (f32[64,512]{1,0:T(8,128)S(1)}, f32[64,512]{1,0:T(8,128)S(1)}, u32[]{:S(2)}, u32[]{:S(2)}) collective-permute-start(f32[64,512]{1,0:T(8,128)S(1)} %get-tuple-element.22), channel_id=1, source_target_pairs={{1,0},{2,1},{3,2},{4,3},{5,4},{6,5},{7,6},{8,7},{9,8},{10,9},{11,1... | collective-permute-start | bytes 393224 | tf_op jit(solution)/shard_map/ppermute | solution.py:17
  75.9 9.3 %collective-permute-start.12 = (f32[64,512]{1,0:T(8,128)S(1)}, f32[64,512]{1,0:T(8,128)S(1)}, u32[]{:S(2)}, u32[]{:S(2)}) collective-permute-start(f32[64,512]{1,0:T(8,128)S(1)} %get-tuple-element.21), channel_id=1, source_target_pairs={{0,1},{1,2},{2,3},{3,4},{4,5},{5,6},{6,7},{7,8},{8,9},{9,10},{10,1... | collective-permute-start | bytes 393224 | tf_op jit(solution)/shard_map/ppermute | solution.py:16
  83.8 3.2 %collective-permute-start.13 = (f32[64,512]{1,0:T(8,128)S(1)}, f32[64,512]{1,0:T(8,128)S(1)}, u32[]{:S(2)}, u32[]{:S(2)}) collective-permute-start(f32[64,512]{1,0:T(8,128)S(1)} %get-tuple-element.20), channel_id=1, source_target_pairs={{1,0},{2,1},{3,2},{4,3},{5,4},{6,5},{7,6},{8,7},{9,8},{10,9},{11,1... | collective-permute-start | bytes 393224 | tf_op jit(solution)/shard_map/ppermute | solution.py:17
  88.3 9.1 %collective-permute-start.14 = (f32[64,512]{1,0:T(8,128)S(1)}, f32[64,512]{1,0:T(8,128)S(1)}, u32[]{:S(2)}, u32[]{:S(2)}) collective-permute-start(f32[64,512]{1,0:T(8,128)S(1)} %get-tuple-element.19), channel_id=1, source_target_pairs={{0,1},{1,2},{2,3},{3,4},{4,5},{5,6},{6,7},{7,8},{8,9},{9,10},{10,1... | collective-permute-start | bytes 393224 | tf_op jit(solution)/shard_map/ppermute | solution.py:16
  96.1 3.2 %collective-permute-start.15 = (f32[64,512]{1,0:T(8,128)S(1)}, f32[64,512]{1,0:T(8,128)S(1)}, u32[]{:S(2)}, u32[]{:S(2)}) collective-permute-start(f32[64,512]{1,0:T(8,128)S(1)} %get-tuple-element.18), channel_id=1, source_target_pairs={{1,0},{2,1},{3,2},{4,3},{5,4},{6,5},{7,6},{8,7},{9,8},{10,9},{11,1... | collective-permute-start | bytes 393224 | tf_op jit(solution)/shard_map/ppermute | solution.py:17
where the time goes:
time: 164 us
  blocking collectives  61.5 us (38%)
  starting transfers between devices  53.4 us (33%)
  matrix products  31.8 us (19%)
  local copies, waits for them, and re-layouts  9.29 us (6%)
  waiting for transfers between devices  6.33 us (4%)
    psum x1, blocking collectives, local(): res_norms = jnp.sqrt(lax.psum(jnp.stack(partials), 'row'))  61.5 us
    ppermute x8, starting transfers between devices, extended(): before = lax.ppermute(last, axis, up)  42.9 us
    dot_general x23, matrix products, matmul(): jnp.dot(left, right, precision=lax.Precision.HIGHEST, preferred_element_t...  31.8 us
    ppermute x8, starting transfers between devices, extended(): after = lax.ppermute(first, axis, down)  10.5 us
    gather x1, local copies, waits for them, and re-layouts, local(): pivots = jnp.diagonal(diag_blocks)[:, None]  8.46 us
    ppermute x8, waiting for transfers between devices, extended(): after = lax.ppermute(first, axis, down)  6.31 us
  transfers between devices with their start and end apart: 16, of which 7 were waited for; matrix products, arithmetic and copies ran while one was open for 18% of the time, Pallas kernels for 0%

commit v1 on v0

--- a/solution.py
+++ b/solution.py
@@ -41,7 +41,7 @@
         local_sums = jnp.sum(residual * residual, axis=0)
         solution = solution + residual / pivots
         partials.append(local_sums)
-    res_norms = jnp.sqrt(lax.psum(jnp.stack(partials), "row"))
+    res_norms = jnp.sqrt(jnp.sum(lax.all_gather(jnp.stack(partials), "row"), axis=0))
     return (solution, res_norms)
 
 

time: 164 us -> 125 us (0.76)
  blocking collectives: 61.5 us -> 22 us
    psum x1 -> x0, blocking collectives: 61.5 us -> none  [local(): res_norms = jnp.sqrt(lax.psum(jnp.stack(partials), 'row'))]
    all_gather x0 -> x1, blocking collectives: none -> 22 us  [local(): lax.all_gather(jnp.stack(partials), 'row')]
  transfers between devices with their start and end apart: 16 -> 16, of which waited for: 7 -> 7; matrix products, arithmetic and copies ran while one was open for 18% -> 24% of each run, Pallas kernels for 0% -> 0%
where the time goes in v1:
time: 125 us; the launch traced here: 124 us
  starting transfers between devices  53.4 us (43%)
  matrix products  31.8 us (25%)
  blocking collectives  22 us (18%)
  local copies, waits for them, and re-layouts  9.29 us (7%)
  waiting for transfers between devices  6.33 us (5%)
    ppermute x8, starting transfers between devices, extended(): before = lax.ppermute(last, axis, up)  42.9 us
    dot_general x23, matrix products, matmul(): jnp.dot(left, right, precision=lax.Precision.HIGHEST, preferred_element_t...  31.8 us
    all_gather x1, blocking collectives, local(): lax.all_gather(jnp.stack(partials), 'row')  22 us
    ppermute x8, starting transfers between devices, extended(): after = lax.ppermute(first, axis, down)  10.5 us
    gather x1, local copies, waits for them, and re-layouts, local(): pivots = jnp.diagonal(diag_blocks)[:, None]  8.46 us
    ppermute x8, waiting for transfers between devices, extended(): after = lax.ppermute(first, axis, down)  6.31 us
  transfers between devices with their start and end apart: 16, of which 7 were waited for; matrix products, arithmetic and copies ran while one was open for 24% of the time, Pallas kernels for 0%

profile of v1, /device:TPU:0, one launch (start us, length us, event | category | flops | bytes accessed | tf_op | source)
XLA Modules:
  0.0 124.1 jit_solution(14763441105539395630)
XLA Ops:
  0.7 1.4 %collective-permute-start.1 = (f32[64,512]{1,0:T(8,128)S(1)}, f32[64,512]{1,0:T(8,128)S(1)}, u32[]{:S(2)}, u32[]{:S(2)}) collective-permute-start(f32[64,512]{1,0:T(8,128)S(1)} %broadcast.16), channel_id=1, source_target_pairs={{1,0},{2,1},{3,2},{4,3},{5,4},{6,5},{7,6},{8,7},{9,8},{10,9},{11,1... | collective-permute-start | bytes 393224 | tf_op jit(solution)/shard_map/ppermute | solution.py:17
  2.1 3.0 %collective-permute-start = (f32[64,512]{1,0:T(8,128)S(1)}, f32[64,512]{1,0:T(8,128)S(1)}, u32[]{:S(2)}, u32[]{:S(2)}) collective-permute-start(f32[64,512]{1,0:T(8,128)S(1)} %broadcast.16), channel_id=1, source_target_pairs={{0,1},{1,2},{2,3},{3,4},{4,5},{5,6},{6,7},{7,8},{8,9},{9,10},{10,1... | collective-permute-start | bytes 393224 | tf_op jit(solution)/shard_map/ppermute | solution.py:16
  5.2 8.5 %gather_fusion = f32[512]{0:T(512)S(1)} fusion(f32[512,512]{1,0:T(8,128)} %param.4, s32[512]{0:T(512)S(1)} %bitcast.89), kind=kCustom, calls=%fused_computation | custom fusion | bytes 8192 | tf_op jit(solution)/shard_map/jit(diagonal)/cond/branch_0_fun/gather | solution.py:27
  14.9 1.2 multiply_reduce_fusion.7
  16.1 4.5 %collective-permute-start.2 = (f32[64,512]{1,0:T(8,128)S(1)}, f32[64,512]{1,0:T(8,128)S(1)}, u32[]{:S(2)}, u32[]{:S(2)}) collective-permute-start(f32[64,512]{1,0:T(8,128)S(1)} %get-tuple-element.31), channel_id=1, source_target_pairs={{0,1},{1,2},{2,3},{3,4},{4,5},{5,6},{6,7},{7,8},{8,9},{9,10},{10,1... | collective-permute-start | bytes 393224 | tf_op jit(solution)/shard_map/ppermute | solution.py:16
  20.6 1.9 %fusion.25 = f32[512,512]{0,1:T(8,128)S(1)} fusion(f32[512,512]{1,0:T(8,128)S(1)} %get-tuple-element.17, f32[512,512]{1,0:T(8,128)S(1)} %copy-done.1), kind=kOutput, calls=%fused_computation.60 | convolution fusion | flops 1610612736 | bytes 3145728 | tf_op jit(solution)/shard_map/dot_general | solution.py:23
  22.5 1.3 %collective-permute-start.3 = (f32[64,512]{1,0:T(8,128)S(1)}, f32[64,512]{1,0:T(8,128)S(1)}, u32[]{:S(2)}, u32[]{:S(2)}) collective-permute-start(f32[64,512]{1,0:T(8,128)S(1)} %get-tuple-element.30), channel_id=1, source_target_pairs={{1,0},{2,1},{3,2},{4,3},{5,4},{6,5},{7,6},{8,7},{9,8},{10,9},{11,1... | collective-permute-start | bytes 393224 | tf_op jit(solution)/shard_map/ppermute | solution.py:17
  25.8 1.2 multiply_reduce_fusion.6
  27.0 5.7 %collective-permute-start.4 = (f32[64,512]{1,0:T(8,128)S(1)}, f32[64,512]{1,0:T(8,128)S(1)}, u32[]{:S(2)}, u32[]{:S(2)}) collective-permute-start(f32[64,512]{1,0:T(8,128)S(1)} %get-tuple-element.29), channel_id=1, source_target_pairs={{0,1},{1,2},{2,3},{3,4},{4,5},{5,6},{6,7},{7,8},{8,9},{9,10},{10,1... | collective-permute-start | bytes 393224 | tf_op jit(solution)/shard_map/ppermute | solution.py:16
  32.7 1.9 %fusion.26 = f32[512,512]{0,1:T(8,128)S(1)} fusion(f32[512,512]{1,0:T(8,128)S(1)} %get-tuple-element.15, f32[512,512]{1,0:T(8,128)S(1)} %copy-done.1), kind=kOutput, calls=%fused_computation.61 | convolution fusion | flops 1610612736 | bytes 3145728 | tf_op jit(solution)/shard_map/dot_general | solution.py:23
  34.6 1.3 %collective-permute-start.5 = (f32[64,512]{1,0:T(8,128)S(1)}, f32[64,512]{1,0:T(8,128)S(1)}, u32[]{:S(2)}, u32[]{:S(2)}) collective-permute-start(f32[64,512]{1,0:T(8,128)S(1)} %get-tuple-element.28), channel_id=1, source_target_pairs={{1,0},{2,1},{3,2},{4,3},{5,4},{6,5},{7,6},{8,7},{9,8},{10,9},{11,1... | collective-permute-start | bytes 393224 | tf_op jit(solution)/shard_map/ppermute | solution.py:17
  37.8 1.2 multiply_reduce_fusion.5
  39.0 6.0 %collective-permute-start.6 = (f32[64,512]{1,0:T(8,128)S(1)}, f32[64,512]{1,0:T(8,128)S(1)}, u32[]{:S(2)}, u32[]{:S(2)}) collective-permute-start(f32[64,512]{1,0:T(8,128)S(1)} %get-tuple-element.27), channel_id=1, source_target_pairs={{0,1},{1,2},{2,3},{3,4},{4,5},{5,6},{6,7},{7,8},{8,9},{9,10},{10,1... | collective-permute-start | bytes 393224 | tf_op jit(solution)/shard_map/ppermute | solution.py:16
  45.1 1.9 %fusion.27 = f32[512,512]{0,1:T(8,128)S(1)} fusion(f32[512,512]{1,0:T(8,128)S(1)} %get-tuple-element.13, f32[512,512]{1,0:T(8,128)S(1)} %copy-done.1), kind=kOutput, calls=%fused_computation.62 | convolution fusion | flops 1610612736 | bytes 3145728 | tf_op jit(solution)/shard_map/dot_general | solution.py:23
  47.0 1.3 %collective-permute-start.7 = (f32[64,512]{1,0:T(8,128)S(1)}, f32[64,512]{1,0:T(8,128)S(1)}, u32[]{:S(2)}, u32[]{:S(2)}) collective-permute-start(f32[64,512]{1,0:T(8,128)S(1)} %get-tuple-element.26), channel_id=1, source_target_pairs={{1,0},{2,1},{3,2},{4,3},{5,4},{6,5},{7,6},{8,7},{9,8},{10,9},{11,1... | collective-permute-start | bytes 393224 | tf_op jit(solution)/shard_map/ppermute | solution.py:17
  51.4 5.9 %collective-permute-start.8 = (f32[64,512]{1,0:T(8,128)S(1)}, f32[64,512]{1,0:T(8,128)S(1)}, u32[]{:S(2)}, u32[]{:S(2)}) collective-permute-start(f32[64,512]{1,0:T(8,128)S(1)} %get-tuple-element.25), channel_id=1, source_target_pairs={{0,1},{1,2},{2,3},{3,4},{4,5},{5,6},{6,7},{7,8},{8,9},{9,10},{10,1... | collective-permute-start | bytes 393224 | tf_op jit(solution)/shard_map/ppermute | solution.py:16
  57.3 1.9 %fusion.28 = f32[512,512]{0,1:T(8,128)S(1)} fusion(f32[512,512]{1,0:T(8,128)S(1)} %get-tuple-element.11, f32[512,512]{1,0:T(8,128)S(1)} %copy-done.1), kind=kOutput, calls=%fused_computation.63 | convolution fusion | flops 1610612736 | bytes 3145728 | tf_op jit(solution)/shard_map/dot_general | solution.py:23
  59.2 1.3 %collective-permute-start.9 = (f32[64,512]{1,0:T(8,128)S(1)}, f32[64,512]{1,0:T(8,128)S(1)}, u32[]{:S(2)}, u32[]{:S(2)}) collective-permute-start(f32[64,512]{1,0:T(8,128)S(1)} %get-tuple-element.24), channel_id=1, source_target_pairs={{1,0},{2,1},{3,2},{4,3},{5,4},{6,5},{7,6},{8,7},{9,8},{10,9},{11,1... | collective-permute-start | bytes 393224 | tf_op jit(solution)/shard_map/ppermute | solution.py:17
  62.4 1.2 multiply_reduce_fusion.3
  63.6 5.9 %collective-permute-start.10 = (f32[64,512]{1,0:T(8,128)S(1)}, f32[64,512]{1,0:T(8,128)S(1)}, u32[]{:S(2)}, u32[]{:S(2)}) collective-permute-start(f32[64,512]{1,0:T(8,128)S(1)} %get-tuple-element.23), channel_id=1, source_target_pairs={{0,1},{1,2},{2,3},{3,4},{4,5},{5,6},{6,7},{7,8},{8,9},{9,10},{10,1... | collective-permute-start | bytes 393224 | tf_op jit(solution)/shard_map/ppermute | solution.py:16
  69.5 1.9 %fusion.29 = f32[512,512]{0,1:T(8,128)S(1)} fusion(f32[512,512]{1,0:T(8,128)S(1)} %get-tuple-element.9, f32[512,512]{1,0:T(8,128)S(1)} %copy-done.1), kind=kOutput, calls=%fused_computation.64 | convolution fusion | flops 1610612736 | bytes 3145728 | tf_op jit(solution)/shard_map/dot_general | solution.py:23
  71.4 1.3 %collective-permute-start.11 = (f32[64,512]{1,0:T(8,128)S(1)}, f32[64,512]{1,0:T(8,128)S(1)}, u32[]{:S(2)}, u32[]{:S(2)}) collective-permute-start(f32[64,512]{1,0:T(8,128)S(1)} %get-tuple-element.22), channel_id=1, source_target_pairs={{1,0},{2,1},{3,2},{4,3},{5,4},{6,5},{7,6},{8,7},{9,8},{10,9},{11,1... | collective-permute-start | bytes 393224 | tf_op jit(solution)/shard_map/ppermute | solution.py:17
  74.6 1.2 multiply_reduce_fusion.2
  75.9 6.1 %collective-permute-start.12 = (f32[64,512]{1,0:T(8,128)S(1)}, f32[64,512]{1,0:T(8,128)S(1)}, u32[]{:S(2)}, u32[]{:S(2)}) collective-permute-start(f32[64,512]{1,0:T(8,128)S(1)} %get-tuple-element.21), channel_id=1, source_target_pairs={{0,1},{1,2},{2,3},{3,4},{4,5},{5,6},{6,7},{7,8},{8,9},{9,10},{10,1... | collective-permute-start | bytes 393224 | tf_op jit(solution)/shard_map/ppermute | solution.py:16
  82.0 1.9 %fusion.30 = f32[512,512]{0,1:T(8,128)S(1)} fusion(f32[512,512]{1,0:T(8,128)S(1)} %get-tuple-element.7, f32[512,512]{1,0:T(8,128)S(1)} %copy-done.1), kind=kOutput, calls=%fused_computation.65 | convolution fusion | flops 1610612736 | bytes 3145728 | tf_op jit(solution)/shard_map/dot_general | solution.py:23
  83.8 1.3 %collective-permute-start.13 = (f32[64,512]{1,0:T(8,128)S(1)}, f32[64,512]{1,0:T(8,128)S(1)}, u32[]{:S(2)}, u32[]{:S(2)}) collective-permute-start(f32[64,512]{1,0:T(8,128)S(1)} %get-tuple-element.20), channel_id=1, source_target_pairs={{1,0},{2,1},{3,2},{4,3},{5,4},{6,5},{7,6},{8,7},{9,8},{10,9},{11,1... | collective-permute-start | bytes 393224 | tf_op jit(solution)/shard_map/ppermute | solution.py:17
  87.1 1.2 multiply_reduce_fusion.1
  88.3 5.9 %collective-permute-start.14 = (f32[64,512]{1,0:T(8,128)S(1)}, f32[64,512]{1,0:T(8,128)S(1)}, u32[]{:S(2)}, u32[]{:S(2)}) collective-permute-start(f32[64,512]{1,0:T(8,128)S(1)} %get-tuple-element.19), channel_id=1, source_target_pairs={{0,1},{1,2},{2,3},{3,4},{4,5},{5,6},{6,7},{7,8},{8,9},{9,10},{10,1... | collective-permute-start | bytes 393224 | tf_op jit(solution)/shard_map/ppermute | solution.py:16
  94.2 1.9 %fusion.31 = f32[512,512]{0,1:T(8,128)S(1)} fusion(f32[512,512]{1,0:T(8,128)S(1)} %get-tuple-element.5, f32[512,512]{1,0:T(8,128)S(1)} %copy-done.1), kind=kOutput, calls=%fused_computation.66 | convolution fusion | flops 1610612736 | bytes 3145728 | tf_op jit(solution)/shard_map/dot_general | solution.py:23
  96.1 1.3 %collective-permute-start.15 = (f32[64,512]{1,0:T(8,128)S(1)}, f32[64,512]{1,0:T(8,128)S(1)}, u32[]{:S(2)}, u32[]{:S(2)}) collective-permute-start(f32[64,512]{1,0:T(8,128)S(1)} %get-tuple-element.18), channel_id=1, source_target_pairs={{1,0},{2,1},{3,2},{4,3},{5,4},{6,5},{7,6},{8,7},{9,8},{10,9},{11,1... | collective-permute-start | bytes 393224 | tf_op jit(solution)/shard_map/ppermute | solution.py:17
  99.3 2.2 %multiply_reduce_fusion = (f32[512]{0:T(512)S(1)}, f32[512,512]{1,0:T(8,128)}) fusion(f32[512,512]{1,0:T(8,128)S(1)} %get-tuple-element.5, f32[512]{0:T(512)S(1)} %gather_fusion, f32[512,512]{1,0:T(8,128)S(1)} %copy-done.3, f32[512,512]{0,1:T(8,128)S(1)} %convolution_add_fusion.1, f32[64,512]{1,0:T(8,128)S(1)} %collective-permute-done.15, ...), kind=kOutput, calls=%fused_computation.33 | convolution fusion | flops 202898944 | bytes 4460544 | tf_op jit(solution)/shard_map/dot_general | solution.py:23
  101.5 22.0 %all-gather = f32[128,512]{1,0:T(8,128)S(1)} all-gather(f32[8,512]{1,0:T(8,128)S(1)} %stack.35), channel_id=2, replica_groups=mesh['grp'=2,'row'=16] {'row'}, dimensions={0}, use_global_device_ids=true | all-gather | bytes 278528 | tf_op jit(solution)/shard_map/all_gather | solution.py:44
  (46 shorter events, 16.7 us)
Async XLA Ops:
  0.6 13.2 %copy-start = (f32[512,64]{0,1:T(8,128)S(1)}, f32[512,64]{0,1:T(8,128)}, u32[]{:S(2)}) copy-start(f32[512,64]{0,1:T(8,128)} %param.6) | copy-start | bytes 393220
  0.7 13.2 %collective-permute-start.1 = (f32[64,512]{1,0:T(8,128)S(1)}, f32[64,512]{1,0:T(8,128)S(1)}, u32[]{:S(2)}, u32[]{:S(2)}) collective-permute-start(f32[64,512]{1,0:T(8,128)S(1)} %broadcast.16), channel_id=1, source_target_pairs={{1,0},{2,1},{3,2},{4,3},{5,4},{6,5},{7,6},{8,7},{9,8},{10,9},{11,1... | collective-permute-start | bytes 393224 | tf_op jit(solution)/shard_map/ppermute | solution.py:17
  2.1 12.8 %collective-permute-start = (f32[64,512]{1,0:T(8,128)S(1)}, f32[64,512]{1,0:T(8,128)S(1)}, u32[]{:S(2)}, u32[]{:S(2)}) collective-permute-start(f32[64,512]{1,0:T(8,128)S(1)} %broadcast.16), channel_id=1, source_target_pairs={{0,1},{1,2},{2,3},{3,4},{4,5},{5,6},{6,7},{7,8},{8,9},{9,10},{10,1... | collective-permute-start | bytes 393224 | tf_op jit(solution)/shard_map/ppermute | solution.py:16
  5.2 8.5 %copy-start.1 = (f32[512,512]{1,0:T(8,128)S(1)}, f32[512,512]{1,0:T(8,128)}, u32[]{:S(2)}) copy-start(f32[512,512]{1,0:T(8,128)} %param.4) | copy-start | bytes 3145732
  13.6 1.2 %copy-start.3 = (f32[512,512]{1,0:T(8,128)S(1)}, f32[512,512]{1,0:T(8,128)}, u32[]{:S(2)}) copy-start(f32[512,512]{1,0:T(8,128)} %param.7) | copy-start | bytes 3145732
  13.8 1.1 copy-start.2
  16.1 7.7 %collective-permute-start.2 = (f32[64,512]{1,0:T(8,128)S(1)}, f32[64,512]{1,0:T(8,128)S(1)}, u32[]{:S(2)}, u32[]{:S(2)}) collective-permute-start(f32[64,512]{1,0:T(8,128)S(1)} %get-tuple-element.31), channel_id=1, source_target_pairs={{0,1},{1,2},{2,3},{3,4},{4,5},{5,6},{6,7},{7,8},{8,9},{9,10},{10,1... | collective-permute-start | bytes 393224 | tf_op jit(solution)/shard_map/ppermute | solution.py:16
  22.5 3.2 %collective-permute-start.3 = (f32[64,512]{1,0:T(8,128)S(1)}, f32[64,512]{1,0:T(8,128)S(1)}, u32[]{:S(2)}, u32[]{:S(2)}) collective-permute-start(f32[64,512]{1,0:T(8,128)S(1)} %get-tuple-element.30), channel_id=1, source_target_pairs={{1,0},{2,1},{3,2},{4,3},{5,4},{6,5},{7,6},{8,7},{9,8},{10,9},{11,1... | collective-permute-start | bytes 393224 | tf_op jit(solution)/shard_map/ppermute | solution.py:17
  27.0 8.9 %collective-permute-start.4 = (f32[64,512]{1,0:T(8,128)S(1)}, f32[64,512]{1,0:T(8,128)S(1)}, u32[]{:S(2)}, u32[]{:S(2)}) collective-permute-start(f32[64,512]{1,0:T(8,128)S(1)} %get-tuple-element.29), channel_id=1, source_target_pairs={{0,1},{1,2},{2,3},{3,4},{4,5},{5,6},{6,7},{7,8},{8,9},{9,10},{10,1... | collective-permute-start | bytes 393224 | tf_op jit(solution)/shard_map/ppermute | solution.py:16
  34.6 3.2 %collective-permute-start.5 = (f32[64,512]{1,0:T(8,128)S(1)}, f32[64,512]{1,0:T(8,128)S(1)}, u32[]{:S(2)}, u32[]{:S(2)}) collective-permute-start(f32[64,512]{1,0:T(8,128)S(1)} %get-tuple-element.28), channel_id=1, source_target_pairs={{1,0},{2,1},{3,2},{4,3},{5,4},{6,5},{7,6},{8,7},{9,8},{10,9},{11,1... | collective-permute-start | bytes 393224 | tf_op jit(solution)/shard_map/ppermute | solution.py:17
  39.0 9.2 %collective-permute-start.6 = (f32[64,512]{1,0:T(8,128)S(1)}, f32[64,512]{1,0:T(8,128)S(1)}, u32[]{:S(2)}, u32[]{:S(2)}) collective-permute-start(f32[64,512]{1,0:T(8,128)S(1)} %get-tuple-element.27), channel_id=1, source_target_pairs={{0,1},{1,2},{2,3},{3,4},{4,5},{5,6},{6,7},{7,8},{8,9},{9,10},{10,1... | collective-permute-start | bytes 393224 | tf_op jit(solution)/shard_map/ppermute | solution.py:16
  47.0 3.2 %collective-permute-start.7 = (f32[64,512]{1,0:T(8,128)S(1)}, f32[64,512]{1,0:T(8,128)S(1)}, u32[]{:S(2)}, u32[]{:S(2)}) collective-permute-start(f32[64,512]{1,0:T(8,128)S(1)} %get-tuple-element.26), channel_id=1, source_target_pairs={{1,0},{2,1},{3,2},{4,3},{5,4},{6,5},{7,6},{8,7},{9,8},{10,9},{11,1... | collective-permute-start | bytes 393224 | tf_op jit(solution)/shard_map/ppermute | solution.py:17
  51.4 9.1 %collective-permute-start.8 = (f32[64,512]{1,0:T(8,128)S(1)}, f32[64,512]{1,0:T(8,128)S(1)}, u32[]{:S(2)}, u32[]{:S(2)}) collective-permute-start(f32[64,512]{1,0:T(8,128)S(1)} %get-tuple-element.25), channel_id=1, source_target_pairs={{0,1},{1,2},{2,3},{3,4},{4,5},{5,6},{6,7},{7,8},{8,9},{9,10},{10,1... | collective-permute-start | bytes 393224 | tf_op jit(solution)/shard_map/ppermute | solution.py:16
  59.2 3.2 %collective-permute-start.9 = (f32[64,512]{1,0:T(8,128)S(1)}, f32[64,512]{1,0:T(8,128)S(1)}, u32[]{:S(2)}, u32[]{:S(2)}) collective-permute-start(f32[64,512]{1,0:T(8,128)S(1)} %get-tuple-element.24), channel_id=1, source_target_pairs={{1,0},{2,1},{3,2},{4,3},{5,4},{6,5},{7,6},{8,7},{9,8},{10,9},{11,1... | collective-permute-start | bytes 393224 | tf_op jit(solution)/shard_map/ppermute | solution.py:17
  63.6 9.1 %collective-permute-start.10 = (f32[64,512]{1,0:T(8,128)S(1)}, f32[64,512]{1,0:T(8,128)S(1)}, u32[]{:S(2)}, u32[]{:S(2)}) collective-permute-start(f32[64,512]{1,0:T(8,128)S(1)} %get-tuple-element.23), channel_id=1, source_target_pairs={{0,1},{1,2},{2,3},{3,4},{4,5},{5,6},{6,7},{7,8},{8,9},{9,10},{10,1... | collective-permute-start | bytes 393224 | tf_op jit(solution)/shard_map/ppermute | solution.py:16
  71.4 3.2 %collective-permute-start.11 = (f32[64,512]{1,0:T(8,128)S(1)}, f32[64,512]{1,0:T(8,128)S(1)}, u32[]{:S(2)}, u32[]{:S(2)}) collective-permute-start(f32[64,512]{1,0:T(8,128)S(1)} %get-tuple-element.22), channel_id=1, source_target_pairs={{1,0},{2,1},{3,2},{4,3},{5,4},{6,5},{7,6},{8,7},{9,8},{10,9},{11,1... | collective-permute-start | bytes 393224 | tf_op jit(solution)/shard_map/ppermute | solution.py:17
  75.9 9.3 %collective-permute-start.12 = (f32[64,512]{1,0:T(8,128)S(1)}, f32[64,512]{1,0:T(8,128)S(1)}, u32[]{:S(2)}, u32[]{:S(2)}) collective-permute-start(f32[64,512]{1,0:T(8,128)S(1)} %get-tuple-element.21), channel_id=1, source_target_pairs={{0,1},{1,2},{2,3},{3,4},{4,5},{5,6},{6,7},{7,8},{8,9},{9,10},{10,1... | collective-permute-start | bytes 393224 | tf_op jit(solution)/shard_map/ppermute | solution.py:16
  83.8 3.2 %collective-permute-start.13 = (f32[64,512]{1,0:T(8,128)S(1)}, f32[64,512]{1,0:T(8,128)S(1)}, u32[]{:S(2)}, u32[]{:S(2)}) collective-permute-start(f32[64,512]{1,0:T(8,128)S(1)} %get-tuple-element.20), channel_id=1, source_target_pairs={{1,0},{2,1},{3,2},{4,3},{5,4},{6,5},{7,6},{8,7},{9,8},{10,9},{11,1... | collective-permute-start | bytes 393224 | tf_op jit(solution)/shard_map/ppermute | solution.py:17
  88.3 9.1 %collective-permute-start.14 = (f32[64,512]{1,0:T(8,128)S(1)}, f32[64,512]{1,0:T(8,128)S(1)}, u32[]{:S(2)}, u32[]{:S(2)}) collective-permute-start(f32[64,512]{1,0:T(8,128)S(1)} %get-tuple-element.19), channel_id=1, source_target_pairs={{0,1},{1,2},{2,3},{3,4},{4,5},{5,6},{6,7},{7,8},{8,9},{9,10},{10,1... | collective-permute-start | bytes 393224 | tf_op jit(solution)/shard_map/ppermute | solution.py:16
  96.1 3.2 %collective-permute-start.15 = (f32[64,512]{1,0:T(8,128)S(1)}, f32[64,512]{1,0:T(8,128)S(1)}, u32[]{:S(2)}, u32[]{:S(2)}) collective-permute-start(f32[64,512]{1,0:T(8,128)S(1)} %get-tuple-element.18), channel_id=1, source_target_pairs={{1,0},{2,1},{3,2},{4,3},{5,4},{6,5},{7,6},{8,7},{9,8},{10,9},{11,1... | collective-permute-start | bytes 393224 | tf_op jit(solution)/shard_map/ppermute | solution.py:17
